TPU v7x, 32 devices: a whole 2x2x4 slice. The times are simulated.
32 devices in a mesh: vx: 4 (over y, x), vy: 8 (over z, core).
Axes of the slice: x: 2, y: 2, z: 4, core: 2. Of those that a mesh axis runs over, the one named last changes fastest.
Arguments:
- tokens: bfloat16 [96, 1, 256, 1024], P(('vx', 'vy')), may hold values from -256 to 256
- var_embed: bfloat16 [91, 1024], replicated, may hold values from -2 to 2
- query: bfloat16 [1024], replicated, may hold values from -6 to 6
- key_weight: bfloat16 [1024, 1024], P('vy'), may hold values from -1 to 1
- value_weight: bfloat16 [1024, 1024], P('vy'), may hold values from -0.1875 to 0.1875
- out_weight: bfloat16 [1024, 1024], P('vy'), may hold values from -0.1875 to 0.1875
- var_slot: int32 [91], replicated, may hold values from 0 to 95, as said below
Outputs:
- aggregated: bfloat16 [1, 256, 1024], P(None, ('vx', 'vy'))
Inputs may be any that keep to these rules, and one draw needn't show every extreme that they name: `var_slot`: distinct slot numbers; at least one device's slot holds a variable.
All inputs are finite; a program needn't handle non-finite values.
Results may differ from a plain program's by a relative error of at most 0.0096.
Values may be sent and summed in bfloat16 or wider, within the bound.
A program may use at most 64 MiB of HBM per device.

v0:
```python
import math
import jax
import jax.numpy as jnp
from jax import lax
from jax.sharding import PartitionSpec as P

HEADS = 16


def attend(keys, values, query_matrix, scale, heads):
    scores = (
        jnp.einsum("vbpd,dh->vbph", keys, query_matrix, preferred_element_type=jnp.float32) * scale
    )
    highest = jnp.max(scores, axis=0, keepdims=True)
    exponent = jnp.exp(scores - highest)
    weights = (exponent / jnp.sum(exponent, axis=0, keepdims=True)).astype(jnp.bfloat16)
    shaped = values.reshape(values.shape[:3] + (heads, values.shape[3] // heads))
    context = jnp.einsum("vbph,vbphe->bphe", weights, shaped, preferred_element_type=jnp.float32)
    return context.astype(jnp.bfloat16).reshape(values.shape[1:])


def shards(tokens, var_embed, query, key_weight, value_weight, out_weight, var_slot):
    slot_dev, batch, patches, width = tokens.shape
    heads = HEADS
    scale = 1.0 / math.sqrt(width // heads)
    count_y = lax.axis_size("vy")
    position = lax.axis_index("vx") * count_y + lax.axis_index("vy")
    local_slots = position * slot_dev + jnp.arange(slot_dev, dtype=jnp.int32)
    slot_match = (local_slots[:, None] == var_slot[None, :]).astype(jnp.bfloat16)
    embed_rows = jnp.dot(slot_match, var_embed, preferred_element_type=jnp.float32)
    mixed = (tokens.astype(jnp.float32) + embed_rows[:, None, None, :]).astype(jnp.bfloat16)
    key_full, value_full = (
        lax.all_gather(key_weight, "vy", axis=0, tiled=True),
        lax.all_gather(value_weight, "vy", axis=0, tiled=True),
    )
    stacked = jnp.stack((key_full, value_full))
    head_of = jnp.arange(width, dtype=jnp.int32) // (width // heads)
    query_matrix = jnp.where(
        head_of[:, None] == jnp.arange(heads, dtype=jnp.int32)[None, :],
        query[:, None],
        jnp.zeros((), jnp.bfloat16),
    )
    outgoing = mixed[None]
    selected = jnp.take(
        lax.all_to_all(outgoing, ("vx", "vy"), split_axis=3, concat_axis=1, tiled=True),
        var_slot,
        axis=1,
    )
    projected = jnp.einsum(
        "vbpd,cde->cvbpe", selected[0], stacked, preferred_element_type=jnp.float32
    ).astype(jnp.bfloat16)
    keys = projected[0]
    values = projected[1]
    context = attend(keys, values, query_matrix, scale, heads)
    flattened = context.reshape(-1, width)
    result = jnp.dot(
        flattened,
        lax.all_gather(out_weight, "vy", axis=0, tiled=True),
        preferred_element_type=jnp.float32,
    )
    return result.astype(jnp.bfloat16).reshape(batch, -1, width)


def solution(mesh):
    placed = (
        P(("vx", "vy"), None, None, None),
        P(),
        P(),
        P("vy", None),
        P("vy", None),
        P("vy", None),
        P(),
    )
    return jax.shard_map(
        shards, mesh=mesh, in_specs=placed, out_specs=P(None, ("vx", "vy"), None), check_vma=False
    )
```

profile of v0, /device:TPU:0, one launch (start us, length us, event | category | flops | bytes accessed | tf_op | source)
XLA Modules:
  0.0 141.9 jit_solution(14651676802304566514)
XLA Ops:
  6.5 0.0 copy-start
  6.5 0.0 all-gather.4.cloned.1.call-start
  6.5 0.7 all-gather.4.cloned.1.call-update
  7.3 0.0 all-gather.6.cloned.1.call-start
  7.3 0.7 all-gather.6.cloned.1.call-update
  8.0 0.0 copy-done
  8.0 0.9 fusion.27
  8.9 4.1 %fusion.5 = bf16[1,3,1,256,1024]{4,1,2,0,3:T(4,128)(2,1)} fusion(bf16[3,1,256,1024]{3,2,1,0:T(8,128)(2,1)} %param.7, f32[3,1024]{1,0:T(4,128)S(1)} %fusion.27), kind=kLoop, calls=%fused_computation.9 | loop fusion | flops 2359296 | bytes 3158016 | tf_op jit(solution)/shard_map/broadcast_in_dim | solution.py:43
  13.0 7.3 %all-to-all-start = ((bf16[1,3,1,256,1024]{4,1,2,0,3:T(4,128)(2,1)}), bf16[1,3,1,256,1024]{4,1,2,0,3:T(4,128)(2,1)S(1)}, u32[]{:S(2)}, u32[]{:S(2)}) async-start(bf16[1,3,1,256,1024]{4,1,2,0,3:T(4,128)(2,1)} %fusion.5), calls=%async_computation | async-start | bytes 4194304 | tf_op jit(solution)/shard_map/all_to_all | solution.py:45
  20.3 0.0 all-gather.8.cloned.1.call-start
  20.4 0.7 all-gather.8.cloned.1.call-update
  21.1 0.0 copy-done.4
  21.1 78.7 %all-to-all-done = bf16[1,3,1,256,1024]{4,1,2,0,3:T(4,128)(2,1)S(1)} async-done(((bf16[1,3,1,256,1024]{4,1,2,0,3:T(4,128)(2,1)}), bf16[1,3,1,256,1024]{4,1,2,0,3:T(4,128)(2,1)S(1)}, u32[]{:S(2)}, u32[]{:S(2)}) %all-to-all-start) | async-done | bytes 1572896 | tf_op jit(solution)/shard_map/all_to_all | solution.py:45
  99.8 0.6 copy.32
  100.4 0.1 copy.18
  100.5 0.7 gather_fusion
  101.3 0.2 broadcast_select_fusion
  101.5 0.0 all-gather.4.cloned.1.call-done
  101.5 1.6 %all-gather.6.cloned.1.call-done = bf16[1024,1024]{1,0:T(8,128)(2,1)} async-done(((bf16[128,1024]{1,0:T(8,128)(2,1)}), bf16[1024,1024]{1,0:T(8,128)(2,1)}) %all-gather.6.cloned.1.call-update) | async-done | bytes 2097168 | tf_op jit(solution)/shard_map/all_gather | solution.py:34
  103.1 6.0 %convert_bitcast_fusion = bf16[2,91,1,8,1024]{4,1,3,0,2:T(8,128)(2,1)S(1)} fusion(bf16[1,1024,1024]{2,1,0:T(8,128)(2,1)} %bitcast.56, bf16[1,1024,1024]{2,1,0:T(8,128)(2,1)} %bitcast.55, bf16[91,8,1024]{2,1,0:T(8,128)(2,1)S(1)} %broadcast_select_fusion), kind=kOutput, calls=%fused_computation.8 | convolution fusion | flops 3063332864 | bytes 8667136 | tf_op jit(solution)/shard_map/vbpd,cde->cvbpe/dot_general | solution.py:49
  109.1 0.0 copy-start.2
  109.1 1.7 %copy-done.2 = bf16[2,91,1,8,1024]{4,1,3,0,2:T(8,128)(2,1)} copy-done((bf16[2,91,1,8,1024]{4,1,3,0,2:T(8,128)(2,1)}, bf16[2,91,1,8,1024]{4,1,3,0,2:T(8,128)(2,1)S(1)}, u32[]{:S(2)}) %copy-start.2) | copy-done | bytes 2981912
  110.8 0.1 slice.11
  110.9 0.0 copy-start.3
  110.9 2.5 %copy.20 = bf16[1,91,1,8,1024]{1,4,3,2,0:T(8,128)(2,1)} copy(bf16[1,91,1,8,1024]{4,1,3,0,2:T(8,128)(2,1)S(1)} %slice.11) | data formatting | bytes 2981888 | tf_op jit(solution)/shard_map/slice | solution.py:53
  113.4 0.0 copy-done.3
  113.5 2.3 %fusion.14 = bf16[91,8,16,1]{0,2,1,3:T(8,128)(2,1)S(1)} fusion(bf16[2,91,1,8,1024]{4,1,3,0,2:T(8,128)(2,1)} %copy-done.2, s32[1024]{0:T(1024)S(1)} %add_select_fusion, bf16[1024]{0:T(1024)(128)(2,1)S(1)} %copy-done.3), kind=kOutput, calls=%fused_computation.21 | convolution fusion | flops 23934900 | bytes 1602304 | tf_op jit(solution)/shard_map/div | solution.py:16
  115.8 0.0 copy-done.1
  115.8 1.2 fusion.16
  117.0 0.1 reshape_reshape.3
  117.1 15.7 %all-gather.8.cloned.1.call-done = bf16[1024,1024]{1,0:T(8,128)(2,1)} async-done(((bf16[128,1024]{1,0:T(8,128)(2,1)}), bf16[1024,1024]{1,0:T(8,128)(2,1)}) %all-gather.8.cloned.1.call-update) | async-done | bytes 2097168 | tf_op jit(solution)/shard_map/all_gather | solution.py:58
  132.7 2.6 %fusion.15 = bf16[1,8,1024]{2,1,0:T(8,128)(2,1)} fusion(bf16[8,1024]{1,0:T(8,128)(2,1)S(1)} %reshape_reshape.3, bf16[1024,1024]{1,0:T(8,128)(2,1)} %all-gather.8.cloned.1.call-done), kind=kOutput, calls=%fused_computation.23 | convolution fusion | flops 16785408 | bytes 2129920 | tf_op jit(solution)/shard_map/dot_general | solution.py:56
  (8 shorter events, 0.0 us)
Async XLA Ops:
  6.5 1.5 %copy-start = (bf16[91,1024]{1,0:T(8,128)(2,1)S(1)}, bf16[91,1024]{1,0:T(8,128)(2,1)}, u32[]{:S(2)}) copy-start(bf16[91,1024]{1,0:T(8,128)(2,1)} %param.8) | copy-start | bytes 559108
  6.5 95.0 %all-gather.4.cloned.1.call-start = ((), (), s32[]{:S(2)}) async-start(), calls=%async_computation.1 | async-start | bytes 2359296 | tf_op jit(solution)/shard_map/all_gather | solution.py:33
  7.3 95.8 %all-gather.6.cloned.1.call-start = ((), (), s32[]{:S(2)}) async-start(), calls=%async_computation.2 | async-start | bytes 2359296 | tf_op jit(solution)/shard_map/all_gather | solution.py:34
  13.0 8.1 %copy-start.4 = (s32[91]{0:T(128)S(1)}, s32[91]{0:T(128)}, u32[]{:S(2)}) copy-start(s32[91]{0:T(128)} %param.13) | copy-start | bytes 1096
  13.0 86.8 %all-to-all-start = ((bf16[1,3,1,256,1024]{4,1,2,0,3:T(4,128)(2,1)}), bf16[1,3,1,256,1024]{4,1,2,0,3:T(4,128)(2,1)S(1)}, u32[]{:S(2)}, u32[]{:S(2)}) async-start(bf16[1,3,1,256,1024]{4,1,2,0,3:T(4,128)(2,1)} %fusion.5), calls=%async_computation | async-start | bytes 4194304 | tf_op jit(solution)/shard_map/all_to_all | solution.py:45
  20.3 112.4 %all-gather.8.cloned.1.call-start = ((), (), s32[]{:S(2)}) async-start(), calls=%async_computation.3 | async-start | bytes 2359296 | tf_op jit(solution)/shard_map/all_gather | solution.py:58
  109.1 1.7 %copy-start.2 = (bf16[2,91,1,8,1024]{4,1,3,0,2:T(8,128)(2,1)}, bf16[2,91,1,8,1024]{4,1,3,0,2:T(8,128)(2,1)S(1)}, u32[]{:S(2)}) copy-start(bf16[2,91,1,8,1024]{4,1,3,0,2:T(8,128)(2,1)S(1)} %convert_bitcast_fusion) | copy-start | bytes 8945668
  110.9 2.5 %copy-start.3 = (bf16[1024]{0:T(1024)(128)(2,1)S(1)}, bf16[1024]{0:T(1024)(128)(2,1)}, u32[]{:S(2)}) copy-start(bf16[1024]{0:T(1024)(128)(2,1)} %param.9) | copy-start | bytes 6148
  113.5 2.3 %copy-start.1 = (bf16[1,91,1,8,1024]{1,4,3,2,0:T(8,128)(2,1)S(1)}, bf16[1,91,1,8,1024]{1,4,3,2,0:T(8,128)(2,1)}, u32[]{:S(2)}) copy-start(bf16[1,91,1,8,1024]{1,4,3,2,0:T(8,128)(2,1)} %copy.20) | copy-start | bytes 4472836
Sparse Core Ops, SparseCore 0:
  8.9 49.8 all-gather.3
  60.4 42.6 all-gather.5
  104.7 28.0 all-gather.7
where the time goes:
time: 142 us
  waiting for transfers between devices  98 us (69%)
  between operations  13.3 us (9%)
  matrix products  13 us (9%)
  starting transfers between devices  7.41 us (5%)
  local copies, waits for them, and re-layouts  5.84 us (4%)
  other arithmetic  4.35 us (3%)
    all_to_all x1, waiting for transfers between devices, shards(): lax.all_to_all(outgoing, ('vx', 'vy'), split_axis=3, concat_axis=1, tiled...  78.7 us
    all_gather x1, waiting for transfers between devices, shards(): lax.all_gather(out_weight, 'vy', axis=0, tiled=True)  15.7 us
    all_to_all x1, starting transfers between devices, shards(): lax.all_to_all(outgoing, ('vx', 'vy'), split_axis=3, concat_axis=1, tiled...  7.33 us
    dot_general x1, matrix products, shards(): jnp.einsum('vbpd,cde->cvbpe', selected[0], stacked, preferred_element_typ...  6.04 us
    broadcast_in_dim x1, other arithmetic, shards(): outgoing = mixed[None]  4.11 us
  transfers between devices with their start and end apart: 4, of which 3 were waited for; matrix products, arithmetic and copies ran while one was open for 13% of the time, Pallas kernels for 0%

commit v1 on v0

--- a/solution.py
+++ b/solution.py
@@ -42,7 +42,15 @@
     )
     outgoing = mixed[None]
     selected = jnp.take(
-        lax.all_to_all(outgoing, ("vx", "vy"), split_axis=3, concat_axis=1, tiled=True),
+        jnp.concatenate(
+            lax.all_to_all(
+                jnp.stack(jnp.split(outgoing, lax.axis_size(("vx", "vy")), axis=3)),
+                ("vx", "vy"),
+                0,
+                0,
+            ),
+            axis=1,
+        ),
         var_slot,
         axis=1,
     )

time: 142 us -> 129 us (0.908)
  waiting for transfers between devices: 98 us -> 67.4 us
  local copies, waits for them, and re-layouts: 5.84 us -> 25.3 us
  other arithmetic: 4.35 us -> 2.35 us
    all_to_all x1, waiting for transfers between devices: 78.7 us -> 54.8 us  [shards(): lax.all_to_all(jnp.stack(jnp.split(outgoing, lax.axis_size(('vx', 'vy')),...]
    unnamed x10 -> x41, local copies, waits for them, and re-layouts: 1.68 us -> 20.8 us
    all_gather x1, waiting for transfers between devices: 15.7 us -> 10.4 us  [shards(): lax.all_gather(out_weight, 'vy', axis=0, tiled=True)]
    div x1 -> x0, matrix products: 2.32 us -> none  [attend(): exponent / jnp.sum(exponent, axis=0, keepdims=True)]
    broadcast_in_dim x1, other arithmetic: 4.11 us -> 1.81 us  [shards(): outgoing = mixed[None]]
    dot_general x0 -> x1, matrix products: none -> 2.18 us  [attend(): jnp.einsum('vbpd,dh->vbph', keys, query_matrix, preferred_element_type=jn...]
    all_gather x1, waiting for transfers between devices: 1.58 us -> 0.02 us  [shards(): lax.all_gather(value_weight, 'vy', axis=0, tiled=True)]
  transfers between devices with their start and end apart: 4 -> 4, of which waited for: 3 -> 2; matrix products, arithmetic and copies ran while one was open for 13% -> 28% of each run, Pallas kernels for 0% -> 0%
where the time goes in v1:
time: 129 us
  waiting for transfers between devices  67.4 us (52%)
  local copies, waits for them, and re-layouts  25.3 us (20%)
  between operations  13.3 us (10%)
  matrix products  12.9 us (10%)
  starting transfers between devices  7.41 us (6%)
  other arithmetic  2.35 us (2%)
    all_to_all x1, waiting for transfers between devices, shards(): lax.all_to_all(jnp.stack(jnp.split(outgoing, lax.axis_size(('vx', 'vy')),...  54.8 us
    unnamed x41, local copies, waits for them, and re-layouts  20.8 us
    all_gather x1, waiting for transfers between devices, shards(): lax.all_gather(out_weight, 'vy', axis=0, tiled=True)  10.4 us
    all_to_all x1, starting transfers between devices, shards(): lax.all_to_all(jnp.stack(jnp.split(outgoing, lax.axis_size(('vx', 'vy')),...  7.33 us
    dot_general x1, matrix products, shards(): jnp.einsum('vbpd,cde->cvbpe', selected[0], stacked, preferred_element_typ...  6.08 us
    slice x2, local copies, waits for them, and re-layouts, shards(): values = projected[1]  2.6 us
    dot_general x1, matrix products, shards(): jnp.dot(flattened, lax.all_gather(out_weight, 'vy', axis=0, tiled=True),...  2.58 us
  transfers between devices with their start and end apart: 4, of which 2 were waited for; matrix products, arithmetic and copies ran while one was open for 28% of the time, Pallas kernels for 0%

profile of v1, /device:TPU:0, one launch (start us, length us, event | category | flops | bytes accessed | tf_op | source)
XLA Modules:
  0.0 128.6 jit_solution(13023215254570947546)
XLA Ops:
  6.5 0.7 all-gather.4.cloned.1.call-update
  7.3 0.7 all-gather.6.cloned.1.call-update
  8.0 0.9 fusion.19
  8.9 1.8 %fusion.3 = bf16[1,3,1,256,1024]{4,3,1,2,0:T(8,128)(2,1)S(1)} fusion(bf16[3,1,256,1024]{3,2,1,0:T(8,128)(2,1)} %param.7, f32[3,1024]{1,0:T(4,128)S(1)} %fusion.19), kind=kLoop, calls=%fused_computation.7 | loop fusion | flops 2359296 | bytes 3158016 | tf_op jit(solution)/shard_map/broadcast_in_dim | solution.py:43
  12.5 0.6 constant_dynamic-update-slice_fusion.28
  13.8 0.6 constant_dynamic-update-slice_fusion.26
  14.4 0.6 constant_dynamic-update-slice_fusion.25
  15.0 0.6 constant_dynamic-update-slice_fusion.24
  16.3 0.6 constant_dynamic-update-slice_fusion.22
  17.5 0.6 constant_dynamic-update-slice_fusion.20
  18.1 0.6 constant_dynamic-update-slice_fusion.19
  18.7 0.6 constant_dynamic-update-slice_fusion.18
  19.4 0.6 constant_dynamic-update-slice_fusion.17
  20.6 0.6 constant_dynamic-update-slice_fusion.15
  24.9 0.6 constant_dynamic-update-slice_fusion.8
  25.5 0.6 constant_dynamic-update-slice_fusion.7
  26.2 0.6 constant_dynamic-update-slice_fusion.6
  26.8 0.6 constant_dynamic-update-slice_fusion.5
  27.4 0.6 constant_dynamic-update-slice_fusion.4
  29.3 0.6 constant_dynamic-update-slice_fusion.1
  29.9 0.6 constant_dynamic-update-slice_fusion
  30.5 7.3 %all-to-all-start = ((bf16[32,1,3,1,8,1024]{5,4,2,3,1,0:T(8,128)(2,1)}), bf16[32,1,3,1,8,1024]{5,4,2,3,1,0:T(8,128)(2,1)S(1)}, u32[]{:S(2)}, u32[]{:S(2)}) async-start(bf16[32,1,3,1,8,1024]{5,4,2,3,1,0:T(8,128)(2,1)} %constant_dynamic-update-slice_fusion), calls=%async_computation | async-start | bytes 3145728 | tf_op jit(solution)/shard_map/all_to_all | solution.py:46
  37.9 0.7 all-gather.8.cloned.1.call-update
  38.7 54.8 %all-to-all-done = bf16[32,1,3,1,8,1024]{5,4,2,3,1,0:T(8,128)(2,1)S(1)} async-done(((bf16[32,1,3,1,8,1024]{5,4,2,3,1,0:T(8,128)(2,1)}), bf16[32,1,3,1,8,1024]{5,4,2,3,1,0:T(8,128)(2,1)S(1)}, u32[]{:S(2)}, u32[]{:S(2)}) %all-to-all-start) | async-done | bytes 1572896 | tf_op jit(solution)/shard_map/all_to_all | solution.py:46
  93.5 0.7 gather_fusion
  94.4 6.1 %convert_bitcast_fusion = bf16[2,91,1,8,1024]{4,1,3,0,2:T(8,128)(2,1)S(1)} fusion(bf16[1,1024,1024]{2,1,0:T(8,128)(2,1)} %bitcast.169, bf16[1,1024,1024]{2,1,0:T(8,128)(2,1)} %bitcast.168, bf16[91,8,1024]{2,1,0:T(8,128)(2,1)S(1)} %broadcast_select_fusion), kind=kOutput, calls=%fused_computation.5 | convolution fusion | flops 3063332864 | bytes 8667136 | tf_op jit(solution)/shard_map/vbpd,cde->cvbpe/dot_general | solution.py:57
  100.5 1.6 %copy-done.2 = bf16[2,91,1,8,1024]{4,1,3,0,2:T(8,128)(2,1)} copy-done((bf16[2,91,1,8,1024]{4,1,3,0,2:T(8,128)(2,1)}, bf16[2,91,1,8,1024]{4,1,3,0,2:T(8,128)(2,1)S(1)}, u32[]{:S(2)}) %copy-start.2) | copy-done | bytes 2981912
  102.3 2.5 %copy.11 = bf16[1,91,1,8,1024]{1,4,3,2,0:T(8,128)(2,1)} copy(bf16[1,91,1,8,1024]{4,1,3,0,2:T(8,128)(2,1)S(1)} %slice.11) | data formatting | bytes 2981888 | tf_op jit(solution)/shard_map/slice | solution.py:61
  104.8 2.2 %fusion.4 = f32[91,8,16]{0,2,1:T(8,128)S(1)} fusion(bf16[2,91,1,8,1024]{4,1,3,0,2:T(8,128)(2,1)} %copy-done.2, s32[1024]{0:T(1024)S(1)} %add_select_fusion, bf16[1024]{0:T(1024)(128)(2,1)S(1)} %copy-done.3), kind=kOutput, calls=%fused_computation.9 | convolution fusion | flops 23887872 | bytes 1625600 | tf_op jit(solution)/shard_map/vbpd,dh->vbph/dot_general | solution.py:12
  107.7 1.2 fusion.25
  109.0 10.4 %all-gather.8.cloned.1.call-done = bf16[1024,1024]{1,0:T(8,128)(2,1)} async-done(((bf16[128,1024]{1,0:T(8,128)(2,1)}), bf16[1024,1024]{1,0:T(8,128)(2,1)}) %all-gather.8.cloned.1.call-update) | async-done | bytes 2097168 | tf_op jit(solution)/shard_map/all_gather | solution.py:66
  119.4 2.6 %fusion.7 = bf16[1,8,1024]{2,1,0:T(8,128)(2,1)} fusion(bf16[8,1024]{1,0:T(8,128)(2,1)S(1)} %reshape_reshape.3, bf16[1024,1024]{1,0:T(8,128)(2,1)} %all-gather.8.cloned.1.call-done), kind=kOutput, calls=%fused_computation.14 | convolution fusion | flops 16785408 | bytes 2129920 | tf_op jit(solution)/shard_map/dot_general | solution.py:64
  (43 shorter events, 10.6 us)
Async XLA Ops:
  6.5 1.5 %copy-start = (bf16[91,1024]{1,0:T(8,128)(2,1)S(1)}, bf16[91,1024]{1,0:T(8,128)(2,1)}, u32[]{:S(2)}) copy-start(bf16[91,1024]{1,0:T(8,128)(2,1)} %param.8) | copy-start | bytes 559108
  6.5 87.9 %all-gather.4.cloned.1.call-start = ((), (), s32[]{:S(2)}) async-start(), calls=%async_computation.1 | async-start | bytes 2359296 | tf_op jit(solution)/shard_map/all_gather | solution.py:33
  7.3 87.2 %all-gather.6.cloned.1.call-start = ((), (), s32[]{:S(2)}) async-start(), calls=%async_computation.2 | async-start | bytes 2359296 | tf_op jit(solution)/shard_map/all_gather | solution.py:34
  30.5 8.1 %copy-start.4 = (s32[91]{0:T(128)S(1)}, s32[91]{0:T(128)}, u32[]{:S(2)}) copy-start(s32[91]{0:T(128)} %param.13) | copy-start | bytes 1096
  30.5 62.9 %all-to-all-start = ((bf16[32,1,3,1,8,1024]{5,4,2,3,1,0:T(8,128)(2,1)}), bf16[32,1,3,1,8,1024]{5,4,2,3,1,0:T(8,128)(2,1)S(1)}, u32[]{:S(2)}, u32[]{:S(2)}) async-start(bf16[32,1,3,1,8,1024]{5,4,2,3,1,0:T(8,128)(2,1)} %constant_dynamic-update-slice_fusion), calls=%async_computation | async-start | bytes 3145728 | tf_op jit(solution)/shard_map/all_to_all | solution.py:46
  37.9 81.6 %all-gather.8.cloned.1.call-start = ((), (), s32[]{:S(2)}) async-start(), calls=%async_computation.3 | async-start | bytes 2359296 | tf_op jit(solution)/shard_map/all_gather | solution.py:66
  100.5 1.6 %copy-start.2 = (bf16[2,91,1,8,1024]{4,1,3,0,2:T(8,128)(2,1)}, bf16[2,91,1,8,1024]{4,1,3,0,2:T(8,128)(2,1)S(1)}, u32[]{:S(2)}) copy-start(bf16[2,91,1,8,1024]{4,1,3,0,2:T(8,128)(2,1)S(1)} %convert_bitcast_fusion) | copy-start | bytes 8945668
  102.3 2.5 %copy-start.3 = (bf16[1024]{0:T(1024)(128)(2,1)S(1)}, bf16[1024]{0:T(1024)(128)(2,1)}, u32[]{:S(2)}) copy-start(bf16[1024]{0:T(1024)(128)(2,1)} %param.9) | copy-start | bytes 6148
  104.8 2.9 %copy-start.1 = (bf16[1,91,1,8,1024]{1,4,3,2,0:T(8,128)(2,1)S(1)}, bf16[1,91,1,8,1024]{1,4,3,2,0:T(8,128)(2,1)}, u32[]{:S(2)}) copy-start(bf16[1,91,1,8,1024]{1,4,3,2,0:T(8,128)(2,1)} %copy.11) | copy-start | bytes 4472836
Sparse Core Ops, SparseCore 0:
  8.9 31.8 all-gather.3
  42.4 47.9 all-gather.5
  92.1 27.3 all-gather.7
